TPU v7x, 32 devices: a whole 2x2x4 slice. The times are simulated.
32 devices in a mesh: section: 4 (over y, x), stem: 8 (over z, core).
Axes of the slice: x: 2, y: 2, z: 4, core: 2. Of those that a mesh axis runs over, the one named last changes fastest.
Arguments:
- bitstrings: int32 [4, 4, 32, 3], P('section'), may hold values 0 or 1
- boundary: float32 [2, 2048], replicated, may hold values from -6 to 6
- stem_tensor: float32 [4, 2, 2048, 8, 2048], P('section', None, 'stem'), may hold values from -0.09375 to 0.09375
- probe_vectors: float32 [4, 2, 2048], P('section'), may hold values from -0.09375 to 0.09375
- inbound_permutations: int32 [4, 2048], replicated, may hold values from 0 to 2047, each once within a row
Outputs:
- amplitudes: float32 [4, 2, 4, 32], P('section')
Inputs may be any that keep to these rules, and one draw needn't show every extreme that they name: `inbound_permutations`: each row of relabeling names every number of 0 to 2047 once.
All inputs are finite; a program needn't handle non-finite values. No bound on the sum of `bitstrings` on one device may be relied on, other than what follows from the above.
Results may differ from a plain program's by a relative error of at most 0.0003.
Values sent between devices are 32-bit elements; how exact they have to be, the bound alone decides.
A program may use at most 128 MiB of HBM per device.

v0:
```python
import jax
import jax.numpy as jnp
from jax import lax
from jax.sharding import PartitionSpec as P

HIGH = lax.Precision.HIGH
HIGHEST = lax.Precision.HIGHEST


def halves(x):
    hi = lax.reduce_precision(x, 8, 7)
    return (hi.astype(jnp.bfloat16), (x - hi).astype(jnp.bfloat16))


def select_columns(x, chosen):
    rows = x.shape[0]
    pick = (jnp.arange(x.shape[1], dtype=jnp.int32)[:, None] == chosen[None, :]).astype(
        jnp.bfloat16
    )
    hi, lo = halves(x)
    both = jnp.dot(jnp.concatenate([hi, lo]), pick, preferred_element_type=jnp.float32)
    return both[:rows] + both[rows:]


def local(bitstrings, boundary, stem_tensor, probe_vectors, inbound_permutations):
    section = lax.axis_index("section")
    sections = lax.axis_size("section")
    rank = lax.axis_index("stem")
    rows, settings, width = stem_tensor.shape[2:]
    bonds = boundary.shape[1]
    micro, batch, qubits = bitstrings.shape[1:]
    count = micro * batch
    powers = jnp.left_shift(jnp.int32(1), jnp.arange(qubits, dtype=jnp.int32))
    own_setting = jnp.sum(bitstrings[0] * powers, axis=-1).reshape(count)
    setting = lax.all_gather(own_setting, "section")
    probe = probe_vectors[0]
    perm = inbound_permutations

    def flat(plane):
        return stem_tensor[0, plane].reshape(rows * settings, width)

    def own_rows(row):
        return lax.dynamic_slice_in_dim(row, rank * rows, rows)

    zeros_a = jnp.zeros((2 * settings, bonds), jnp.float32)

    def first_forward():
        t_re, t_im = (stem_tensor[0, 0], stem_tensor[0, 1])
        b = jnp.dot(
            boundary,
            (jnp.arange(bonds, dtype=jnp.int32)[:, None] == own_rows(perm[0])[None, :]).astype(
                jnp.float32
            ),
            precision=HIGHEST,
        )
        b_re, b_im = (b[0][:, None, None], b[1][:, None, None])
        u_re = jnp.sum(b_re * t_re - b_im * t_im, axis=0)
        u_im = jnp.sum(b_re * t_im + b_im * t_re, axis=0)
        return jnp.concatenate([u_re, u_im])

    def last_backward():
        t_re, t_im = (stem_tensor[0, 0], stem_tensor[0, 1])
        v_re = jnp.sum(t_re * probe[0] - t_im * probe[1], axis=-1)
        v_im = jnp.sum(t_re * probe[1] + t_im * probe[0], axis=-1)
        v = jnp.concatenate([v_re.T, v_im.T])
        return lax.dynamic_update_slice_in_dim(zeros_a, v, rank * rows, 1)

    idle = lambda: zeros_a
    vectors = lax.switch(section, [first_forward, idle, idle, last_backward])

    def product_with_probe(v_re, v_im):
        return (
            jnp.dot(v_re, probe[0], precision=HIGHEST) - jnp.dot(v_im, probe[1], precision=HIGHEST),
            jnp.dot(v_re, probe[1], precision=HIGHEST) + jnp.dot(v_im, probe[0], precision=HIGHEST),
        )

    amp_first = jnp.stack(product_with_probe(vectors[:settings], vectors[settings:]))
    moved = lax.ppermute(vectors, "section", [(0, 1), (3, 2)])
    vectors = lax.psum(moved, "stem")
    ends = settings + 1
    pairs = settings * settings
    zeros_u = jnp.zeros((2 * pairs, bonds), jnp.float32)
    zeros_w = jnp.zeros((rows, settings * 2 * ends), jnp.float32)
    zeros_p = jnp.zeros((2, pairs), jnp.float32)

    def second_forward():
        x = select_columns(vectors, own_rows(perm[1])).reshape(2, settings, 1, rows, 1)
        same = jnp.eye(settings, dtype=jnp.float32).reshape(1, 1, settings, 1, settings)
        spread = (x * same).reshape(2 * pairs, rows * settings)
        p_re = jnp.dot(spread, flat(0), precision=HIGH)
        p_im = jnp.dot(spread, flat(1), precision=HIGH)
        u_re = p_re[:pairs] - p_im[pairs:]
        u_im = p_im[:pairs] + p_re[pairs:]
        amp = jnp.stack(product_with_probe(u_re, u_im))
        u = select_columns(jnp.concatenate([u_re, u_im]), perm[2])
        return (u, zeros_w, amp)

    def second_backward():
        place = (perm[3][:, None] == jnp.arange(bonds, dtype=jnp.int32)[None, :]).astype(
            jnp.bfloat16
        )
        hi, lo = halves(vectors)
        both = jnp.dot(jnp.concatenate([hi, lo]), place, preferred_element_type=jnp.float32)
        v = (both[: 2 * settings] + both[2 * settings :]).reshape(2, settings, bonds)
        v = jnp.concatenate([v, probe[:, None, :]], axis=1).reshape(2 * ends, bonds)
        q_re = lax.dot_general(flat(0), v, (((1,), (1,)), ((), ())), precision=HIGH)
        q_im = lax.dot_general(flat(1), v, (((1,), (1,)), ((), ())), precision=HIGH)
        w_re = q_re[:, :ends] - q_im[:, ends:]
        w_im = q_re[:, ends:] + q_im[:, :ends]
        w = jnp.concatenate([w_re, w_im], axis=1).reshape(rows, settings * 2 * ends)
        return (zeros_u, w, zeros_p)

    none = lambda: (zeros_u, zeros_w, zeros_p)
    u, w, amp_second = lax.switch(section, [none, second_forward, second_backward, none])
    w = lax.ppermute(w, "section", [(2, 1)])
    w = lax.all_gather(w, "stem", axis=0, tiled=True)
    joined = jnp.dot(u, w, precision=HIGH).reshape(2, pairs, settings, 2, ends)
    j_re = (joined[0, :, :, 0] - joined[1, :, :, 1]).reshape(pairs, settings * ends)
    j_im = (joined[0, :, :, 1] + joined[1, :, :, 0]).reshape(pairs, settings * ends)
    onehot = lambda ids, size: (ids[:, None] == jnp.arange(size, dtype=jnp.int32)[None, :]).astype(
        jnp.float32
    )
    front = onehot(setting[0] * settings + setting[1], pairs)
    first = jnp.dot(amp_first, onehot(setting[0], settings).T, precision=HIGHEST)
    first = jnp.where(section == 0, first, 0.0)
    second = jnp.dot(amp_second, front.T, precision=HIGHEST)
    third_pick = onehot(setting[2] * ends + settings, settings * ends)
    fourth_pick = onehot(setting[2] * ends + setting[3], settings * ends)
    rows_re = jnp.dot(front, j_re, precision=HIGHEST)
    rows_im = jnp.dot(front, j_im, precision=HIGHEST)
    third = jnp.stack(
        [jnp.sum(rows_re * third_pick, axis=1), jnp.sum(rows_im * third_pick, axis=1)]
    )
    fourth = jnp.stack(
        [jnp.sum(rows_re * fourth_pick, axis=1), jnp.sum(rows_im * fourth_pick, axis=1)]
    )
    partial = jnp.stack([first, second, third, fourth])
    total = lax.psum(partial, ("section", "stem"))
    own = lax.dynamic_index_in_dim(total, section, 0, False)
    return own.reshape(1, 2, micro, batch)


def solution(mesh):
    return jax.shard_map(
        local,
        mesh=mesh,
        in_specs=(
            P("section", None, None, None),
            P(),
            P("section", None, "stem", None, None),
            P("section", None, None),
            P(),
        ),
        out_specs=P("section", None, None, None),
        check_vma=False,
    )
```

profile of v0, /device:TPU:0, one launch (start us, length us, event | category | flops | bytes accessed | tf_op | source)
XLA Modules:
  0.0 223.1 jit_solution(2156276009823240268)
XLA Ops:
  6.5 15.1 %conditional.2 = (f32[16,2048]{1,0:T(8,128)}, f32[8,2048]{1,0:T(8,128)S(1)}, f32[8,2048]{1,0:T(8,128)S(1)}) conditional(s32[]{:T(128)} %clamp.4, (s32[4,2048]{1,0:T(4,128)}, s32[]{:T(128)}, f32[2,2048]{1,0:T(2,128)}, f32[1,2,256,8,2048]{4,3,2,1,0:T(8,128)}) %tuple.41, () %tuple.42, () %tuple.43, ...), branch_computations={%region_0.3_spmd, %region_3.4_spmd, %region_4.0_spmd, %region_5.8_... | conditional | flops 46661636 | bytes 34078796 | solution.py:69
  6.5 0.8 slice.108
  7.3 1.4 fusion.5
  8.8 12.2 %fusion.1 = (f32[8,2048]{1,0:T(8,128)S(1)}, f32[8,2048]{1,0:T(8,128)S(1)}) fusion(f32[1,2,256,8,2048]{4,3,2,1,0:T(8,128)} %get-tuple-element.43, f32[256]{0:T(256)S(1)} %bitcast.210, f32[256]{0:T(256)S(1)} %bitcast.209), kind=kLoop, calls=%fused_computation.3 | loop fusion | flops 33521664 | bytes 33687552 | tf_op jit(solution)/shard_map/cond/branch_0_fun/reduce_sum | solution.py:57
  21.0 0.6 pad_maximum_fusion
  21.6 1.3 collective-permute-start
  22.9 4.0 %collective-permute-done = f32[16,2048]{1,0:T(8,128)S(1)} collective-permute-done((f32[16,2048]{1,0:T(8,128)}, f32[16,2048]{1,0:T(8,128)S(1)}, u32[]{:S(2)}, u32[]{:S(2)}) %collective-permute-start) | collective-permute-done | bytes 131104 | tf_op jit(solution)/shard_map/ppermute | solution.py:78
  26.9 0.6 copy-done.3
  27.6 58.5 %all-reduce.2.cloned.1.call-done = f32[16,2048]{1,0:T(8,128)} async-done(((f32[16,2048]{1,0:T(8,128)}), f32[16,2048]{1,0:T(8,128)}) %all-reduce.2.cloned.1.call-update) | async-done | bytes 131088 | tf_op jit(solution)/shard_map/psum | solution.py:79
  86.1 0.4 conditional.3
  86.5 0.7 collective-permute-start.1
  87.2 0.7 copy-done.2
  88.1 63.0 %all-gather = s32[4,1,128]{2,1,0:T(1,128)S(1)} all-gather(s32[1,1,128]{2,1,0:T(1,128)S(1)} %reshape.101), channel_id=1, replica_groups=mesh['section'=4,'stem'=8] {'section'}, dimensions={0}, use_global_device_ids=true | all-gather | bytes 2560 | tf_op jit(solution)/shard_map/all_gather | solution.py:35
  151.1 0.9 convolution_bitcast_fusion.7
  152.1 0.3 convolution_bitcast_fusion.5
  152.3 0.3 fusion.67
  152.6 0.3 fusion.69
  153.1 0.3 convolution_bitcast_fusion.4
  153.4 17.8 %all-gather.3.cloned.1.call-done = f32[2048,144]{1,0:T(8,128)} async-done(((f32[256,144]{1,0:T(8,128)}), f32[2048,144]{1,0:T(8,128)}) %all-gather.3.cloned.1.call-update) | async-done | bytes 1179664 | tf_op jit(solution)/shard_map/all_gather | solution.py:116
  171.1 3.4 %fusion.95 = f32[128,144]{0,1:T(8,128)S(1)} fusion(f32[128,2048]{1,0:T(8,128)S(1)} %get-tuple-element.66, f32[2048,144]{1,0:T(8,128)} %all-gather.3.cloned.1.call-done), kind=kOutput, calls=%fused_computation.158 | convolution fusion | flops 226492416 | bytes 2301952 | tf_op jit(solution)/shard_map/dot_general | solution.py:117
  174.7 0.3 fusion.71
  175.0 0.3 select_reduce_fusion.2
  175.4 40.2 %psum.15 = f32[4,2,128]{2,1,0:T(2,128)S(1)} all-reduce(f32[4,2,128]{2,1,0:T(2,128)S(1)} %pad_maximum_fusion.5), channel_id=1, replica_groups=mesh['section'=4,'stem'=8] {'section','stem'}, use_global_device_ids=true, to_apply=%region_18.19 | all-reduce | flops 1024 | bytes 8192 | tf_op jit(solution)/shard_map/psum | solution.py:138
  215.5 0.7 reshape.100
  (27 shorter events, 0.8 us)
Async XLA Ops:
  6.5 79.5 %all-reduce.2.cloned.1.call-start = ((), (), s32[]{:S(2)}) async-start(), calls=%async_computation | async-start | bytes 262144 | tf_op jit(solution)/shard_map/psum | solution.py:79
  21.6 5.3 %collective-permute-start = (f32[16,2048]{1,0:T(8,128)}, f32[16,2048]{1,0:T(8,128)S(1)}, u32[]{:S(2)}, u32[]{:S(2)}) collective-permute-start(f32[16,2048]{1,0:T(8,128)} %get-tuple-element.64), channel_id=1, source_target_pairs={{0,8},{24,16},{1,9},{25,17},{2,10},{26,18},{3,11},{27,19},{4,12},{... | collective-permute-start | bytes 393224 | tf_op jit(solution)/shard_map/ppermute | solution.py:78
  26.9 0.6 copy-start.3
  27.6 143.6 %all-gather.3.cloned.1.call-start = ((), (), s32[]{:S(2)}) async-start(), calls=%async_computation.1 | async-start | bytes 2359296 | tf_op jit(solution)/shard_map/all_gather | solution.py:116
  86.1 1.9 copy-start.4
  86.1 66.0 %copy-start = (f32[1,2,2048]{2,1,0:T(2,128)S(1)}, f32[1,2,2048]{2,1,0:T(2,128)}, u32[]{:S(2)}) copy-start(f32[1,2,2048]{2,1,0:T(2,128)} %param.16) | copy-start | bytes 49156
  86.5 0.7 collective-permute-start.1
  87.2 0.7 copy-start.2
Sparse Core Ops, SparseCore 0:
  27.7 58.3 all-reduce.1
  88.0 83.0 all-gather.2
where the time goes:
time: 224 us; the launch traced here: 223 us
  blocking collectives  103 us (46%)
  waiting for transfers between devices  80.3 us (36%)
  between operations  13.5 us (6%)
  other arithmetic  13.1 us (6%)
  matrix products  7.6 us (3%)
  local copies, waits for them, and re-layouts  3.15 us (1%)
    all_gather x1, blocking collectives, local(): setting = lax.all_gather(own_setting, 'section')  63 us
    psum x1, waiting for transfers between devices, local(): vectors = lax.psum(moved, 'stem')  58.5 us
    psum x1, blocking collectives, local(): total = lax.psum(partial, ('section', 'stem'))  40.2 us
    all_gather x1, waiting for transfers between devices, local(): w = lax.all_gather(w, 'stem', axis=0, tiled=True)  17.8 us
    reduce_sum x1, other arithmetic, first_forward(): u_re = jnp.sum(b_re * t_re - b_im * t_im, axis=0)  12.2 us
  transfers between devices with their start and end apart: 4, of which 3 were waited for; matrix products, arithmetic and copies ran while one was open for 1% of the time, Pallas kernels for 0%

commit v1 on v0

--- a/solution.py
+++ b/solution.py
@@ -135,7 +135,8 @@
         [jnp.sum(rows_re * fourth_pick, axis=1), jnp.sum(rows_im * fourth_pick, axis=1)]
     )
     partial = jnp.stack([first, second, third, fourth])
-    total = lax.psum(partial, ("section", "stem"))
+    parts = lax.all_gather(partial, ("section", "stem"))
+    total = jnp.sum(parts, axis=0)
     own = lax.dynamic_index_in_dim(total, section, 0, False)
     return own.reshape(1, 2, micro, batch)
 

time: 224 us -> 224 us (level)
    all_gather x0 -> x1, blocking collectives: none -> 40.5 us  [local(): parts = lax.all_gather(partial, ('section', 'stem'))]
    psum x1 -> x0, blocking collectives: 40.2 us -> none  [local(): total = lax.psum(partial, ('section', 'stem'))]
where the time goes in v1:
time: 224 us; the launch traced here: 223 us
  blocking collectives  103 us (46%)
  waiting for transfers between devices  80.3 us (36%)
  between operations  13.5 us (6%)
  other arithmetic  13.1 us (6%)
  matrix products  7.6 us (3%)
  local copies, waits for them, and re-layouts  3.15 us (1%)
    all_gather x1, blocking collectives, local(): setting = lax.all_gather(own_setting, 'section')  63 us
    psum x1, waiting for transfers between devices, local(): vectors = lax.psum(moved, 'stem')  58.5 us
    all_gather x1, blocking collectives, local(): parts = lax.all_gather(partial, ('section', 'stem'))  40.5 us
    all_gather x1, waiting for transfers between devices, local(): w = lax.all_gather(w, 'stem', axis=0, tiled=True)  17.8 us
    reduce_sum x1, other arithmetic, first_forward(): u_re = jnp.sum(b_re * t_re - b_im * t_im, axis=0)  12.2 us
  transfers between devices with their start and end apart: 4, of which 3 were waited for; matrix products, arithmetic and copies ran while one was open for 1% of the time, Pallas kernels for 0%

profile of v1, /device:TPU:0, one launch (start us, length us, event | category | flops | bytes accessed | tf_op | source)
XLA Modules:
  0.0 223.4 jit_solution(9189706416662337775)
XLA Ops:
  6.5 15.1 %conditional.2 = (f32[16,2048]{1,0:T(8,128)}, f32[8,2048]{1,0:T(8,128)S(1)}, f32[8,2048]{1,0:T(8,128)S(1)}) conditional(s32[]{:T(128)} %clamp.4, (s32[4,2048]{1,0:T(4,128)}, s32[]{:T(128)}, f32[2,2048]{1,0:T(2,128)}, f32[1,2,256,8,2048]{4,3,2,1,0:T(8,128)}) %tuple.41, () %tuple.42, () %tuple.43, ...), branch_computations={%region_0.3_spmd, %region_3.4_spmd, %region_4.0_spmd, %region_5.8_... | conditional | flops 46661636 | bytes 34078796 | solution.py:69
  6.5 0.8 slice.108
  7.3 1.4 fusion.5
  8.8 12.2 %fusion.1 = (f32[8,2048]{1,0:T(8,128)S(1)}, f32[8,2048]{1,0:T(8,128)S(1)}) fusion(f32[1,2,256,8,2048]{4,3,2,1,0:T(8,128)} %get-tuple-element.43, f32[256]{0:T(256)S(1)} %bitcast.212, f32[256]{0:T(256)S(1)} %bitcast.211), kind=kLoop, calls=%fused_computation.3 | loop fusion | flops 33521664 | bytes 33687552 | tf_op jit(solution)/shard_map/cond/branch_0_fun/reduce_sum | solution.py:57
  21.0 0.6 pad_maximum_fusion
  21.6 1.3 collective-permute-start
  22.9 4.0 %collective-permute-done = f32[16,2048]{1,0:T(8,128)S(1)} collective-permute-done((f32[16,2048]{1,0:T(8,128)}, f32[16,2048]{1,0:T(8,128)S(1)}, u32[]{:S(2)}, u32[]{:S(2)}) %collective-permute-start) | collective-permute-done | bytes 131104 | tf_op jit(solution)/shard_map/ppermute | solution.py:78
  26.9 0.6 copy-done.3
  27.6 58.5 %all-reduce.2.cloned.1.call-done = f32[16,2048]{1,0:T(8,128)} async-done(((f32[16,2048]{1,0:T(8,128)}), f32[16,2048]{1,0:T(8,128)}) %all-reduce.2.cloned.1.call-update) | async-done | bytes 131088 | tf_op jit(solution)/shard_map/psum | solution.py:79
  86.1 0.4 conditional.3
  86.5 0.7 collective-permute-start.1
  87.2 0.7 copy-done.2
  88.1 63.0 %all-gather.1 = s32[4,1,128]{2,1,0:T(1,128)S(1)} all-gather(s32[1,1,128]{2,1,0:T(1,128)S(1)} %reshape.102), channel_id=1, replica_groups=mesh['section'=4,'stem'=8] {'section'}, dimensions={0}, use_global_device_ids=true | all-gather | bytes 2560 | tf_op jit(solution)/shard_map/all_gather | solution.py:35
  151.1 0.9 convolution_bitcast_fusion.7
  152.1 0.3 convolution_bitcast_fusion.5
  152.3 0.3 fusion.67
  152.6 0.3 fusion.69
  153.1 0.3 convolution_bitcast_fusion.4
  153.4 17.8 %all-gather.4.cloned.1.call-done = f32[2048,144]{1,0:T(8,128)} async-done(((f32[256,144]{1,0:T(8,128)}), f32[2048,144]{1,0:T(8,128)}) %all-gather.4.cloned.1.call-update) | async-done | bytes 1179664 | tf_op jit(solution)/shard_map/all_gather | solution.py:116
  171.1 3.4 %fusion.95 = f32[128,144]{0,1:T(8,128)S(1)} fusion(f32[128,2048]{1,0:T(8,128)S(1)} %get-tuple-element.66, f32[2048,144]{1,0:T(8,128)} %all-gather.4.cloned.1.call-done), kind=kOutput, calls=%fused_computation.158 | convolution fusion | flops 226492416 | bytes 2301952 | tf_op jit(solution)/shard_map/dot_general | solution.py:117
  174.7 0.3 fusion.71
  175.0 0.3 select_reduce_fusion.2
  175.4 40.5 %all-gather = f32[128,2,128]{2,1,0:T(2,128)S(1)} all-gather(f32[4,2,128]{2,1,0:T(2,128)S(1)} %pad_maximum_fusion.5), channel_id=2, replica_groups=mesh['section'=4,'stem'=8] {'section','stem'}, dimensions={0}, use_global_device_ids=true | all-gather | bytes 135168 | tf_op jit(solution)/shard_map/all_gather | solution.py:138
  215.9 0.7 reshape.100
  (28 shorter events, 0.9 us)
Async XLA Ops:
  6.5 79.5 %all-reduce.2.cloned.1.call-start = ((), (), s32[]{:S(2)}) async-start(), calls=%async_computation | async-start | bytes 262144 | tf_op jit(solution)/shard_map/psum | solution.py:79
  21.6 5.3 %collective-permute-start = (f32[16,2048]{1,0:T(8,128)}, f32[16,2048]{1,0:T(8,128)S(1)}, u32[]{:S(2)}, u32[]{:S(2)}) collective-permute-start(f32[16,2048]{1,0:T(8,128)} %get-tuple-element.64), channel_id=1, source_target_pairs={{0,8},{24,16},{1,9},{25,17},{2,10},{26,18},{3,11},{27,19},{4,12},{... | collective-permute-start | bytes 393224 | tf_op jit(solution)/shard_map/ppermute | solution.py:78
  26.9 0.6 copy-start.3
  27.6 143.6 %all-gather.4.cloned.1.call-start = ((), (), s32[]{:S(2)}) async-start(), calls=%async_computation.1 | async-start | bytes 2359296 | tf_op jit(solution)/shard_map/all_gather | solution.py:116
  86.1 1.9 copy-start.4
  86.1 66.0 %copy-start = (f32[1,2,2048]{2,1,0:T(2,128)S(1)}, f32[1,2,2048]{2,1,0:T(2,128)}, u32[]{:S(2)}) copy-start(f32[1,2,2048]{2,1,0:T(2,128)} %param.16) | copy-start | bytes 49156
  86.5 0.7 collective-permute-start.1
  87.2 0.7 copy-start.2
Sparse Core Ops, SparseCore 0:
  27.7 58.3 all-reduce.1
  88.0 83.0 all-gather.3

commit v2 on v0

--- a/solution.py
+++ b/solution.py
@@ -135,7 +135,8 @@
         [jnp.sum(rows_re * fourth_pick, axis=1), jnp.sum(rows_im * fourth_pick, axis=1)]
     )
     partial = jnp.stack([first, second, third, fourth])
-    total = lax.psum(partial, ("section", "stem"))
+    half = lax.psum(partial, "stem")
+    total = lax.psum(half, "section")
     own = lax.dynamic_index_in_dim(total, section, 0, False)
     return own.reshape(1, 2, micro, batch)
 

time: 224 us -> 208 us (0.929)
  blocking collectives: 103 us -> 88.1 us
    psum x1 -> x2, blocking collectives: 40.2 us -> 25.1 us  [the longest x1 15.3 us: local(): half = lax.psum(partial, 'stem')]
where the time goes in v2:
time: 208 us
  blocking collectives  88.1 us (42%)
  waiting for transfers between devices  80.2 us (39%)
  between operations  13.5 us (6%)
  other arithmetic  13.1 us (6%)
  matrix products  7.6 us (4%)
  local copies, waits for them, and re-layouts  3.15 us (2%)
    all_gather x1, blocking collectives, local(): setting = lax.all_gather(own_setting, 'section')  63 us
    psum x1, waiting for transfers between devices, local(): vectors = lax.psum(moved, 'stem')  58.4 us
    all_gather x1, waiting for transfers between devices, local(): w = lax.all_gather(w, 'stem', axis=0, tiled=True)  17.8 us
    psum x1, blocking collectives, local(): half = lax.psum(partial, 'stem')  15.3 us
    reduce_sum x1, other arithmetic, first_forward(): u_re = jnp.sum(b_re * t_re - b_im * t_im, axis=0)  12.2 us
    psum x1, blocking collectives, local(): total = lax.psum(half, 'section')  9.84 us
  transfers between devices with their start and end apart: 4, of which 3 were waited for; matrix products, arithmetic and copies ran while one was open for 1% of the time, Pallas kernels for 0%

profile of v2, /device:TPU:0, one launch (start us, length us, event | category | flops | bytes accessed | tf_op | source)
XLA Modules:
  0.0 208.0 jit_solution(15354438021009770072)
XLA Ops:
  6.5 15.1 %conditional.2 = (f32[16,2048]{1,0:T(8,128)}, f32[8,2048]{1,0:T(8,128)S(1)}, f32[8,2048]{1,0:T(8,128)S(1)}) conditional(s32[]{:T(128)} %clamp.4, (s32[4,2048]{1,0:T(4,128)}, s32[]{:T(128)}, f32[2,2048]{1,0:T(2,128)}, f32[1,2,256,8,2048]{4,3,2,1,0:T(8,128)}) %tuple.41, () %tuple.42, () %tuple.43, ...), branch_computations={%region_0.3_spmd, %region_3.4_spmd, %region_4.0_spmd, %region_5.8_... | conditional | flops 46661636 | bytes 34078796 | solution.py:69
  6.5 0.8 slice.108
  7.3 1.4 fusion.5
  8.8 12.2 %fusion.1 = (f32[8,2048]{1,0:T(8,128)S(1)}, f32[8,2048]{1,0:T(8,128)S(1)}) fusion(f32[1,2,256,8,2048]{4,3,2,1,0:T(8,128)} %get-tuple-element.43, f32[256]{0:T(256)S(1)} %bitcast.210, f32[256]{0:T(256)S(1)} %bitcast.209), kind=kLoop, calls=%fused_computation.3 | loop fusion | flops 33521664 | bytes 33687552 | tf_op jit(solution)/shard_map/cond/branch_0_fun/reduce_sum | solution.py:57
  21.0 0.6 pad_maximum_fusion
  21.6 1.3 collective-permute-start
  22.9 4.0 %collective-permute-done = f32[16,2048]{1,0:T(8,128)S(1)} collective-permute-done((f32[16,2048]{1,0:T(8,128)}, f32[16,2048]{1,0:T(8,128)S(1)}, u32[]{:S(2)}, u32[]{:S(2)}) %collective-permute-start) | collective-permute-done | bytes 131104 | tf_op jit(solution)/shard_map/ppermute | solution.py:78
  26.9 0.6 copy-done.3
  27.6 58.4 %all-reduce.2.cloned.1.call-done = f32[16,2048]{1,0:T(8,128)} async-done(((f32[16,2048]{1,0:T(8,128)}), f32[16,2048]{1,0:T(8,128)}) %all-reduce.2.cloned.1.call-update) | async-done | bytes 131088 | tf_op jit(solution)/shard_map/psum | solution.py:79
  86.1 0.4 conditional.3
  86.4 0.7 collective-permute-start.1
  87.1 0.7 copy-done.2
  88.1 63.0 %all-gather = s32[4,1,128]{2,1,0:T(1,128)S(1)} all-gather(s32[1,1,128]{2,1,0:T(1,128)S(1)} %reshape.101), channel_id=1, replica_groups=mesh['section'=4,'stem'=8] {'section'}, dimensions={0}, use_global_device_ids=true | all-gather | bytes 2560 | tf_op jit(solution)/shard_map/all_gather | solution.py:35
  151.1 0.9 convolution_bitcast_fusion.7
  152.3 0.3 fusion.67
  152.5 0.3 fusion.69
  153.0 0.3 convolution_bitcast_fusion.4
  153.3 17.8 %all-gather.3.cloned.1.call-done = f32[2048,144]{1,0:T(8,128)} async-done(((f32[256,144]{1,0:T(8,128)}), f32[2048,144]{1,0:T(8,128)}) %all-gather.3.cloned.1.call-update) | async-done | bytes 1179664 | tf_op jit(solution)/shard_map/all_gather | solution.py:116
  171.1 3.4 %fusion.95 = f32[128,144]{0,1:T(8,128)S(1)} fusion(f32[128,2048]{1,0:T(8,128)S(1)} %get-tuple-element.66, f32[2048,144]{1,0:T(8,128)} %all-gather.3.cloned.1.call-done), kind=kOutput, calls=%fused_computation.158 | convolution fusion | flops 226492416 | bytes 2301952 | tf_op jit(solution)/shard_map/dot_general | solution.py:117
  174.7 0.3 fusion.71
  175.0 0.3 select_reduce_fusion.2
  175.3 15.3 %psum.22 = f32[4,2,128]{2,1,0:T(2,128)S(1)} all-reduce(f32[4,2,128]{2,1,0:T(2,128)S(1)} %pad_maximum_fusion.5), channel_id=1, replica_groups=mesh['section'=4,'stem'=8] {'stem'}, use_global_device_ids=true, to_apply=%region_18.19 | all-reduce | flops 1024 | bytes 8192 | tf_op jit(solution)/shard_map/psum | solution.py:138
  190.6 9.8 %psum.23 = f32[4,2,128]{2,1,0:T(2,128)S(1)} all-reduce(f32[4,2,128]{2,1,0:T(2,128)S(1)} %psum.22), channel_id=1, replica_groups=mesh['section'=4,'stem'=8] {'section'}, use_global_device_ids=true, to_apply=%region_19.20 | all-reduce | flops 1024 | bytes 8192 | tf_op jit(solution)/shard_map/psum | solution.py:139
  200.4 0.7 reshape.100
  (28 shorter events, 1.1 us)
Async XLA Ops:
  6.5 79.5 %all-reduce.2.cloned.1.call-start = ((), (), s32[]{:S(2)}) async-start(), calls=%async_computation | async-start | bytes 262144 | tf_op jit(solution)/shard_map/psum | solution.py:79
  21.6 5.3 %collective-permute-start = (f32[16,2048]{1,0:T(8,128)}, f32[16,2048]{1,0:T(8,128)S(1)}, u32[]{:S(2)}, u32[]{:S(2)}) collective-permute-start(f32[16,2048]{1,0:T(8,128)} %get-tuple-element.64), channel_id=1, source_target_pairs={{0,8},{24,16},{1,9},{25,17},{2,10},{26,18},{3,11},{27,19},{4,12},{... | collective-permute-start | bytes 393224 | tf_op jit(solution)/shard_map/ppermute | solution.py:78
  26.9 0.6 copy-start.3
  27.6 143.5 %all-gather.3.cloned.1.call-start = ((), (), s32[]{:S(2)}) async-start(), calls=%async_computation.1 | async-start | bytes 2359296 | tf_op jit(solution)/shard_map/all_gather | solution.py:116
  86.1 1.8 copy-start.4
  86.1 66.0 %copy-start = (f32[1,2,2048]{2,1,0:T(2,128)S(1)}, f32[1,2,2048]{2,1,0:T(2,128)}, u32[]{:S(2)}) copy-start(f32[1,2,2048]{2,1,0:T(2,128)} %param.16) | copy-start | bytes 49156
  86.4 0.7 collective-permute-start.1
  87.1 0.7 copy-start.2
Sparse Core Ops, SparseCore 0:
  27.7 58.3 all-reduce.1
  88.0 83.0 all-gather.2
